TPU v7x, 32 devices: a whole 2x2x4 slice. The times are simulated.
32 devices in a mesh: win: 4 (over y, x), dof: 8 (over z, core).
Axes of the slice: x: 2, y: 2, z: 4, core: 2. Of those that a mesh axis runs over, the one named last changes fastest.
Arguments:
- snapshots: bfloat16 [262144, 256], P('dof', 'win'), may hold values from -6 to 6
- sketch_matrix: bfloat16 [262144, 128], P('dof'), may hold values from -0.01171875 to 0.01171875
- pivots: int32 [8, 64], P('win'), may hold values from 0 to 127
Outputs:
- singular: float32 [8, 64], P('win')
- projections: float32 [8, 64, 32], P('win')
All inputs are finite; a program needn't handle non-finite values.
Results may differ from a plain program's by a relative error of at most 0.0003.
Values sent between devices are 32-bit elements; how exact they have to be, the bound alone decides.
No kernel may reach another device: no remote copies, remote signals or barrier semaphores. Data moves between devices by JAX's collectives and lax.ppermute only.
A program may use at most 64 MiB of HBM per device.

v0:
```python
import math
import jax
import jax.numpy as jnp
from jax import lax
from jax.sharding import PartitionSpec as P

RANK = 64
ORTH_ITERS = 2
HIGHEST_PREC = lax.Precision.HIGHEST


def orthogonal(prefix_grams):
    batch_count = prefix_grams.shape[0]
    sketch_width = prefix_grams.shape[1]
    basis_cols = jnp.broadcast_to(
        jnp.eye(sketch_width, RANK, dtype=jnp.float32), (batch_count, sketch_width, RANK)
    )
    for sweep_index in range(ORTH_ITERS):
        images = jnp.einsum("wij,wjk->wik", prefix_grams, basis_cols, precision=HIGHEST_PREC)
        inner_gram = jnp.einsum("wik,wil->wkl", images, images, precision=HIGHEST_PREC)
        chol_factor = jnp.linalg.cholesky(inner_gram)
        solved = jax.scipy.linalg.solve_triangular(
            chol_factor, jnp.swapaxes(images, 1, 2), lower=True
        )
        basis_cols = jnp.swapaxes(solved, 1, 2)
    return basis_cols


def finish(prefix_grams, basis_cols, window_blocks, pivots):
    images = jnp.einsum("wij,wjk->wik", prefix_grams, basis_cols, precision=HIGHEST_PREC)
    singular = jnp.sqrt(jnp.sum(basis_cols * images, axis=1))
    sketch_width = basis_cols.shape[1]
    pivot_table = (
        pivots[:, :, None] == jnp.arange(sketch_width, dtype=jnp.int32)[None, None, :]
    ).astype(jnp.float32)
    pivot_weight = jnp.einsum(
        "wrk,wkr->wr", pivot_table, basis_cols, precision=HIGHEST_PREC
    ) * math.sqrt(sketch_width)
    projections = (
        jnp.einsum("wkr,wks->wrs", basis_cols, window_blocks, precision=HIGHEST_PREC)
        * pivot_weight[:, :, None]
    )
    return (singular, projections)


def masked_gram(gathered, limit):
    column_ids = lax.iota(jnp.int32, gathered.shape[1])
    keep_mask = (column_ids < limit).astype(jnp.float32)
    return jnp.dot(gathered * keep_mask[None, :], gathered.T, precision=HIGHEST_PREC)


def local(snapshots, sketch_matrix, pivots):
    windows_here = pivots.shape[0]
    sketch_width = sketch_matrix.shape[1]
    local_cols = snapshots.shape[1]
    snap_count = local_cols // windows_here
    win_position = lax.axis_index("win")
    partial_value = lax.dot_general(
        sketch_matrix, snapshots, (((0,), (0,)), ((), ())), preferred_element_type=jnp.float32
    )
    coefficients = lax.psum(partial_value, "dof")
    window_blocks = jnp.transpose(
        coefficients.reshape(sketch_width, windows_here, snap_count), (1, 0, 2)
    )
    window_grams = jnp.einsum("wks,wjs->wkj", window_blocks, window_blocks, precision=HIGHEST_PREC)
    own_prefix = jnp.cumsum(window_grams, axis=0)
    gathered = lax.all_gather(coefficients, "win", axis=1, tiled=True)
    earlier = masked_gram(gathered, win_position * local_cols)
    window_ids = win_position * windows_here + jnp.arange(windows_here, dtype=jnp.int32)
    snap_totals = (snap_count * (window_ids + 1)).astype(jnp.float32)
    identity = jnp.eye(sketch_width, dtype=jnp.float32)
    prefix_grams = identity[None] + (earlier[None] + own_prefix) / snap_totals[:, None, None]
    basis_cols = orthogonal(prefix_grams)
    singular, projections = finish(prefix_grams, basis_cols, window_blocks, pivots)
    return (singular, projections)


def solution(mesh):
    placed = (P("dof", "win"), P("dof", None), P("win", None))
    return jax.shard_map(
        local,
        mesh=mesh,
        in_specs=placed,
        out_specs=(P("win", None), P("win", None, None)),
        check_vma=False,
    )
```

profile of v0, /device:TPU:0, one launch (start us, length us, event | category | flops | bytes accessed | tf_op | source)
XLA Modules:
  0.0 94.3 jit_solution(17351688111466763597)
XLA Ops:
  0.6 0.0 copy-start
  0.6 6.2 %fusion.22 = f32[128,64]{0,1:T(8,128)S(1)} fusion(bf16[32768,64]{0,1:T(8,128)(2,1)} %param.6, bf16[32768,128]{1,0:T(8,128)(2,1)} %param.7), kind=kOutput, calls=%fused_computation.42 | convolution fusion | flops 536870912 | bytes 12615680 | tf_op jit(solution)/shard_map/dot_general | solution.py:58
  6.9 30.3 %psum.7 = f32[128,64]{0,1:T(8,128)S(1)} all-reduce(f32[128,64]{0,1:T(8,128)S(1)} %fusion.22), channel_id=1, replica_groups=mesh['win'=4,'dof'=8] {'dof'}, use_global_device_ids=true, to_apply=%region_0.0 | all-reduce | flops 8192 | bytes 65536 | tf_op jit(solution)/shard_map/psum | solution.py:61
  37.2 8.4 %all_gather.3 = f32[128,256]{0,1:T(8,128)S(1)} all-gather(f32[128,64]{0,1:T(8,128)S(1)} %psum.7), channel_id=1, replica_groups=mesh['win'=4,'dof'=8] {'win'}, dimensions={1}, use_global_device_ids=true | all-gather | bytes 163840 | tf_op jit(solution)/shard_map/all_gather | solution.py:67
  45.6 0.5 fusion.3
  46.1 0.4 fusion.18
  46.5 0.1 fusion.1
  46.6 0.4 fusion.15
  47.0 0.2 fusion.19
  47.2 0.1 copy.8
  47.3 11.7 %custom-call.8 = f32[2,64,64]{2,1,0:T(8,128)S(1)} custom-call(f32[2,64,64]{2,1,0:T(8,128)S(1)} %fusion.12), custom_call_target="Cholesky" | custom-call | tf_op jit(solution)/shard_map/jit(cholesky)/cholesky | solution.py:21
  59.1 0.1 compare_reduce_fusion.1
  59.3 0.1 select_bitcast_fusion.1
  59.3 9.8 %custom-call.9 = f32[2,1,64,64]{2,3,1,0:T(8,128)S(1)} custom-call(f32[2,1,64,64]{3,2,1,0:T(8,128)S(1)} %select_bitcast_fusion.1), custom_call_target="InvertDiagBlocksLowerTriangular" | custom-call | tf_op jit(solution)/shard_map/jit(_solve_triangular)/vmap()/triangular_solve | solution.py:22
  69.2 0.3 fusion.9
  69.5 0.4 fusion.20
  69.8 0.2 fusion.21
  70.1 0.1 copy.9
  70.2 11.7 %custom-call.10 = f32[2,64,64]{2,1,0:T(8,128)S(1)} custom-call(f32[2,64,64]{2,1,0:T(8,128)S(1)} %fusion.8), custom_call_target="Cholesky" | custom-call | tf_op jit(solution)/shard_map/jit(cholesky)/cholesky | solution.py:21
  82.0 0.1 compare_reduce_fusion
  82.1 0.1 select_bitcast_fusion
  82.2 9.8 %custom-call.11 = f32[2,1,64,64]{2,3,1,0:T(8,128)S(1)} custom-call(f32[2,1,64,64]{3,2,1,0:T(8,128)S(1)} %select_bitcast_fusion), custom_call_target="InvertDiagBlocksLowerTriangular" | custom-call | tf_op jit(solution)/shard_map/jit(_solve_triangular)/vmap()/triangular_solve | solution.py:22
  92.0 0.0 copy-done
  92.0 0.4 select_reduce_fusion
  92.4 0.8 convolution_multiply_fusion.1
  93.2 0.4 fusion.2
  93.7 0.6 sqrt.3
  (11 shorter events, 0.1 us)
Async XLA Ops:
  0.6 91.4 %copy-start = (s32[2,64]{1,0:T(2,128)S(1)}, s32[2,64]{1,0:T(2,128)}, u32[]{:S(2)}) copy-start(s32[2,64]{1,0:T(2,128)} %param.8) | copy-start | bytes 1540
where the time goes:
time: 94.5 us; the launch traced here: 94.3 us
  other arithmetic  43.7 us (46%)
  blocking collectives  38.7 us (41%)
  matrix products  10.2 us (11%)
    psum x1, blocking collectives, local(): coefficients = lax.psum(partial_value, 'dof')  30.3 us
    another operation x7, other arithmetic, orthogonal(): chol_factor = jnp.linalg.cholesky(inner_gram)  23.8 us
    another operation x5, other arithmetic, orthogonal(): jax.scipy.linalg.solve_triangular(chol_factor, jnp.swapaxes(images, 1, 2)...  19.8 us
    all_gather x1, blocking collectives, local(): gathered = lax.all_gather(coefficients, 'win', axis=1, tiled=True)  8.45 us
    dot_general x1, matrix products, local(): lax.dot_general(sketch_matrix, snapshots, (((0,), (0,)), ((), ())), prefe...  6.24 us

commit v1 on v0

--- a/solution.py
+++ b/solution.py
@@ -58,7 +58,8 @@
     partial_value = lax.dot_general(
         sketch_matrix, snapshots, (((0,), (0,)), ((), ())), preferred_element_type=jnp.float32
     )
-    coefficients = lax.psum(partial_value, "dof")
+    parts = lax.all_gather(partial_value, "dof", axis=0, tiled=False)
+    coefficients = parts.sum(axis=0)
     window_blocks = jnp.transpose(
         coefficients.reshape(sketch_width, windows_here, snap_count), (1, 0, 2)
     )

time: 94.5 us -> 80.2 us (0.85)
  blocking collectives: 38.7 us -> 24.4 us
    psum x1 -> x0, blocking collectives: 30.3 us -> none  [local(): coefficients = lax.psum(partial_value, 'dof')]
    all_gather x0 -> x1, blocking collectives: none -> 15.9 us  [local(): parts = lax.all_gather(partial_value, 'dof', axis=0, tiled=False)]
where the time goes in v1:
time: 80.2 us; the launch traced here: 80 us
  other arithmetic  43.8 us (55%)
  blocking collectives  24.4 us (30%)
  matrix products  10.2 us (13%)
  between operations  0.82 us (1%)
    another operation x7, other arithmetic, orthogonal(): chol_factor = jnp.linalg.cholesky(inner_gram)  23.8 us
    another operation x5, other arithmetic, orthogonal(): jax.scipy.linalg.solve_triangular(chol_factor, jnp.swapaxes(images, 1, 2)...  19.8 us
    all_gather x1, blocking collectives, local(): parts = lax.all_gather(partial_value, 'dof', axis=0, tiled=False)  15.9 us
    all_gather x1, blocking collectives, local(): gathered = lax.all_gather(coefficients, 'win', axis=1, tiled=True)  8.47 us
    dot_general x1, matrix products, local(): lax.dot_general(sketch_matrix, snapshots, (((0,), (0,)), ((), ())), prefe...  6.24 us

profile of v1, /device:TPU:0, one launch (start us, length us, event | category | flops | bytes accessed | tf_op | source)
XLA Modules:
  0.0 80.0 jit_solution(4856855974704492232)
XLA Ops:
  0.6 0.0 copy-start
  0.6 6.2 %fusion.22 = f32[128,64]{0,1:T(8,128)S(1)} fusion(bf16[32768,64]{0,1:T(8,128)(2,1)} %param.6, bf16[32768,128]{1,0:T(8,128)(2,1)} %param.7), kind=kOutput, calls=%fused_computation.43 | convolution fusion | flops 536870912 | bytes 12615680 | tf_op jit(solution)/shard_map/dot_general | solution.py:58
  6.9 15.9 %all-gather = f32[1024,64]{0,1:T(8,128)S(1)} all-gather(f32[128,64]{0,1:T(8,128)S(1)} %fusion.22), channel_id=2, replica_groups=mesh['win'=4,'dof'=8] {'dof'}, dimensions={0}, use_global_device_ids=true | all-gather | bytes 294912 | tf_op jit(solution)/shard_map/all_gather | solution.py:61
  22.9 0.1 bitcast_reduce_fusion
  22.9 8.5 %all_gather.11 = f32[128,256]{0,1:T(8,128)S(1)} all-gather(f32[128,64]{0,1:T(8,128)S(1)} %bitcast_reduce_fusion), channel_id=1, replica_groups=mesh['win'=4,'dof'=8] {'win'}, dimensions={1}, use_global_device_ids=true | all-gather | bytes 163840 | tf_op jit(solution)/shard_map/all_gather | solution.py:68
  31.4 0.5 fusion.3
  31.9 0.4 fusion.18
  32.3 0.1 fusion.1
  32.4 0.4 fusion.15
  32.8 0.2 fusion.19
  33.0 0.1 copy.8
  33.1 11.7 %custom-call.8 = f32[2,64,64]{2,1,0:T(8,128)S(1)} custom-call(f32[2,64,64]{2,1,0:T(8,128)S(1)} %fusion.12), custom_call_target="Cholesky" | custom-call | tf_op jit(solution)/shard_map/jit(cholesky)/cholesky | solution.py:21
  44.9 0.1 compare_reduce_fusion.1
  45.0 0.1 select_bitcast_fusion.1
  45.1 9.8 %custom-call.9 = f32[2,1,64,64]{2,3,1,0:T(8,128)S(1)} custom-call(f32[2,1,64,64]{3,2,1,0:T(8,128)S(1)} %select_bitcast_fusion.1), custom_call_target="InvertDiagBlocksLowerTriangular" | custom-call | tf_op jit(solution)/shard_map/jit(_solve_triangular)/vmap()/triangular_solve | solution.py:22
  54.9 0.3 fusion.9
  55.2 0.4 fusion.20
  55.6 0.2 fusion.21
  55.8 0.1 copy.9
  55.9 11.7 %custom-call.10 = f32[2,64,64]{2,1,0:T(8,128)S(1)} custom-call(f32[2,64,64]{2,1,0:T(8,128)S(1)} %fusion.8), custom_call_target="Cholesky" | custom-call | tf_op jit(solution)/shard_map/jit(cholesky)/cholesky | solution.py:21
  67.7 0.1 compare_reduce_fusion
  67.8 0.1 select_bitcast_fusion
  67.9 9.8 %custom-call.11 = f32[2,1,64,64]{2,3,1,0:T(8,128)S(1)} custom-call(f32[2,1,64,64]{3,2,1,0:T(8,128)S(1)} %select_bitcast_fusion), custom_call_target="InvertDiagBlocksLowerTriangular" | custom-call | tf_op jit(solution)/shard_map/jit(_solve_triangular)/vmap()/triangular_solve | solution.py:22
  77.7 0.0 copy-done
  77.8 0.4 select_reduce_fusion
  78.2 0.8 %convolution_multiply_fusion.1 = f32[2,64,32]{1,2,0:T(8,128)} fusion(f32[2,64,128]{2,1,0:T(8,128)S(1)} %get-tuple-element.5, f32[2,128,32]{1,2,0:T(8,128)S(1)} %bitcast.59, f32[2,64]{1,0:T(2,128)S(1)} %broadcast_multiply_fusion), kind=kOutput, calls=%fused_computation.5 | convolution fusion | flops 6295552 | bytes 115200 | tf_op jit(solution)/shard_map/wkr,wks->wrs/dot_general | solution.py:40
  79.0 0.4 fusion.2
  79.4 0.6 sqrt.3
  (12 shorter events, 0.2 us)
Async XLA Ops:
  0.6 77.1 %copy-start = (s32[2,64]{1,0:T(2,128)S(1)}, s32[2,64]{1,0:T(2,128)}, u32[]{:S(2)}) copy-start(s32[2,64]{1,0:T(2,128)} %param.8) | copy-start | bytes 1540
